TPU v7x, 32 devices: a whole 2x2x4 slice. The times are simulated.
32 devices in a mesh: blk: 8 (over z, x), rows: 4 (over y, core).
Axes of the slice: x: 2, y: 2, z: 4, core: 2. Of those that a mesh axis runs over, the one named last changes fastest.
Arguments:
- columns: float32 [512, 16384], P('blk', 'rows'), may hold values from -100 to 100
- plan: int32 [3, 16], replicated, may hold values from 0 to 15, as said below
Outputs:
- swept: float32 [512, 16384], P('blk', 'rows')
- off_ratio: float32 [3], replicated
Inputs may be any that keep to these rules, and one draw needn't show every extreme that they name: `plan`: row s is a permutation of the 16 positions (position k is slot k % 2 of blk index k // 2). In each row there are a slot t and a number m of 1 to 7 such that the block in slot t of every blk index i goes to slot t of blk index (i + m) modulo 16 / 2, and every other block stays where it is.
All inputs are finite; a program needn't handle non-finite values. Where the computation divides by a largest or mean magnitude, that divisor is 1e-20 or more.
Results may differ from a plain program's by a relative error of at most 0.00011.
Values sent between devices are 32-bit elements; how exact they have to be, the bound alone decides.
A program may use at most 64 MiB of HBM per device.

v0:
```python
from functools import partial

import jax
import jax.numpy as jnp
from jax import lax
from jax.experimental import pallas as pl
from jax.experimental.pallas import tpu as pltpu
from jax.sharding import PartitionSpec as P

EIG_ITERS = 3
NS_ITERS = 8
CHUNKS = 2
NEAR_PART = 9
MESH = pl.DeviceIdType.MESH


def split(value):
    high = value.astype(jnp.bfloat16)
    low = (value - high.astype(jnp.float32)).astype(jnp.bfloat16)
    return high, low


def left_of(value):
    high = value.astype(jnp.bfloat16).astype(jnp.float32)
    low = value - high
    lane = lax.broadcasted_iota(jnp.int32, value.shape, 1)
    mixed = jnp.where(lane < value.shape[1] // 2, high, low).astype(jnp.bfloat16)
    return jnp.concatenate([mixed, mixed], axis=1)


def right_of(value):
    high, low = split(value)
    return jnp.concatenate([high, high, low, low], axis=0)


def dot(left, right):
    return jnp.dot(left, right, preferred_element_type=jnp.float32)


def orthonormal(z, zt):
    y = z / jnp.sqrt(jnp.sum(z * z, axis=0, keepdims=True))
    t = zt / jnp.sqrt(0.5 * jnp.sum(zt * zt, axis=1, keepdims=True))
    inner = dot(left_of(t), right_of(y))
    bound = jnp.max(jnp.sum(jnp.abs(inner), axis=0, keepdims=True), axis=1, keepdims=True)
    root = jnp.sqrt(bound)
    y = y / root
    t = t / root

    def turn(_, carry):
        y, t = carry
        inner = dot(left_of(t), right_of(y))
        y_next = 1.5 * y - 0.5 * dot(left_of(y), right_of(inner))
        t_next = 1.5 * t - 0.5 * dot(left_of(inner), right_of(t))
        return y_next, t_next

    return lax.fori_loop(0, NS_ITERS, turn, (y, t))


def early_share(share, distance, count):
    part = 4 if 4 * distance > count and 4 * distance < 3 * count else NEAR_PART
    return max(share * part // 16 // 256 * 256, 256)


def step_kernel(step, last, distance, plan_ref, current_ref, *refs):
    seen_ref = refs[0] if step else None
    (out_ref, stat_ref, grams, sums, early, turning, turning_in, leaving,
     send_sem, recv_sem, stat_send, stat_recv, move_send, move_recv) = refs[1 if step else 0:]
    width, share = current_ref.shape
    half = width // 2
    count = lax.axis_size("rows")
    others = lax.axis_size("blk")
    me = lax.axis_index("rows")
    mine = lax.axis_index("blk")
    target = lax.rem(mine + distance, others)
    source = lax.rem(mine + others - distance, others)
    early_lanes = early.shape[1]
    chunk = leaving.shape[1] // CHUNKS

    barrier = pltpu.get_barrier_semaphore()
    for offset in range(1, count):
        peer = lax.rem(me + offset, count)
        pl.semaphore_signal(barrier, inc=1, device_id={"rows": peer}, device_id_type=MESH)
    greeted = count - 1
    if last:
        for offset in range(1, others):
            peer = lax.rem(mine + offset, others)
            pl.semaphore_signal(barrier, inc=1, device_id={"blk": peer}, device_id_type=MESH)
        greeted += others - 1
    else:
        for peer in (target, source):
            pl.semaphore_signal(barrier, inc=1, device_id={"blk": peer}, device_id_type=MESH)
        greeted += 2
    def forward(src, dst, index):
        copy = pltpu.make_async_remote_copy(
            src_ref=src, dst_ref=dst,
            send_sem=move_send.at[index], recv_sem=move_recv.at[index],
            device_id={"blk": target}, device_id_type=MESH)
        copy.start()
        return copy

    high, low = split(current_ref[...])
    stacked = jnp.concatenate([high, low], axis=0)
    products = lax.dot_general(stacked, stacked, (((1,), (1,)), ((), ())),
                               preferred_element_type=jnp.float32)
    folded = products + pltpu.roll(products, width, 1)
    gram = folded[:width] + folded[width:]
    lane = lax.broadcasted_iota(jnp.int32, (half, 2 * width), 1)
    grams[me] = jnp.where(lane < width, gram[:half], gram[half:])

    pl.semaphore_wait(barrier, greeted)
    copies = []
    for offset in range(1, count):
        peer = lax.rem(me + offset, count)
        copy = pltpu.make_async_remote_copy(
            src_ref=grams.at[me], dst_ref=grams.at[me],
            send_sem=send_sem.at[offset - 1], recv_sem=recv_sem.at[offset - 1],
            device_id={"rows": peer}, device_id_type=MESH)
        copy.start()
        copies.append(copy)
    early_copy = forward(current_ref.at[:, pl.ds(0, early_lanes)], early, 0)
    for copy in copies:
        copy.wait()
    packed = grams[0]
    for index in range(1, count):
        packed = packed + grams[index]
    turned = pltpu.roll(packed, width, 1)
    gram = jnp.concatenate([jnp.where(lane < width, packed, turned),
                            jnp.where(lane < width, turned, packed)], axis=0)

    row = lax.broadcasted_iota(jnp.int32, gram.shape, 0)
    column = lax.broadcasted_iota(jnp.int32, gram.shape, 1)
    square = gram * gram
    diag_part = jnp.where(row == column, square, 0.0)
    off_part = jnp.where((row == column) | (column >= width), 0.0, square)
    off_total = jnp.sum(jnp.sum(off_part, axis=0, keepdims=True), axis=1, keepdims=True)
    diag_total = jnp.sum(jnp.sum(diag_part, axis=0, keepdims=True), axis=1, keepdims=True)
    line = lax.broadcasted_iota(jnp.int32, stat_ref.shape, 0)
    at_lane = lax.broadcasted_iota(jnp.int32, stat_ref.shape, 1)
    fresh = jnp.where(line == 0, off_total, diag_total)
    before = seen_ref[...] if step else jnp.zeros(stat_ref.shape, jnp.float32)
    totals = jnp.where((at_lane == step) & (line < 2), fresh, before)
    stat_copies = []
    if last:
        sums[mine] = totals
        for offset in range(1, others):
            peer = lax.rem(mine + offset, others)
            copy = pltpu.make_async_remote_copy(
                src_ref=sums.at[mine], dst_ref=sums.at[mine],
                send_sem=stat_send.at[offset - 1], recv_sem=stat_recv.at[offset - 1],
                device_id={"blk": peer}, device_id_type=MESH)
            copy.start()
            stat_copies.append(copy)
    else:
        stat_ref[...] = totals

    q, t = orthonormal(gram, gram)
    gram_left, gram_right = left_of(gram), right_of(gram)

    def again(_, carry):
        q, t = carry
        return orthonormal(dot(gram_left, right_of(q)), dot(left_of(t), gram_right))

    q, t = lax.fori_loop(1, EIG_ITERS, again, (q, t))

    leaving_slot = jnp.where(plan_ref[step, 1] != 1, 1, 0)
    second_slot = 1 if step == 0 else jnp.where(plan_ref[step - 1, 1] != 1, 1, 0)
    leaving_last = leaving_slot == second_slot
    t_stay = jnp.where(leaving_last, t[:half], t[half:])
    t_move = jnp.where(leaving_last, t[half:], t[:half])
    turning[...] = t_move
    turn_copy = forward(turning, turning_in, 1)
    left = left_of(jnp.concatenate([t_stay, t_move], axis=0))
    moves = []
    for index in range(CHUNKS):
        where = pl.ds(early_lanes + index * chunk, chunk)
        there = pl.ds(index * chunk, chunk)
        rotated = dot(left, right_of(current_ref[:, where]))
        leaving[:, there] = rotated[half:]
        moves.append(forward(leaving.at[:, there], out_ref.at[pl.ds(half, half), where], 2 + index))
        out_ref[pl.ds(0, half), where] = rotated[:half]
    left_stay = left_of(t_stay)
    piece = 256
    for start in range(0, early_lanes, piece):
        where = pl.ds(start, piece)
        out_ref[pl.ds(0, half), where] = dot(left_stay, right_of(current_ref[:, where]))

    early_copy.wait()
    turn_copy.wait()
    left_move = left_of(turning_in[...])
    for start in range(0, early_lanes, piece):
        where = pl.ds(start, piece)
        out_ref[pl.ds(half, half), where] = dot(left_move, right_of(early[:, where]))

    if last:
        for copy in stat_copies:
            copy.wait()
        total = sums[0]
        for index in range(1, others):
            total = total + sums[index]
        ratio = jnp.sqrt(total[0:1]) / jnp.sqrt(total[1:2])
        stat_ref[...] = jnp.broadcast_to(ratio, stat_ref.shape)
    for copy in moves:
        copy.wait()


def step_call(plan, current, *seen, step, last, distance):
    width, share = current.shape
    half = width // 2
    count = lax.axis_size("rows")
    others = lax.axis_size("blk")
    early_lanes = early_share(share, distance, others)
    vmem = pl.BlockSpec(memory_space=pltpu.VMEM)
    return pl.pallas_call(
        partial(step_kernel, step, last, distance),
        out_shape=(
            jax.ShapeDtypeStruct(current.shape, jnp.float32),
            jax.ShapeDtypeStruct((8, 128), jnp.float32),
        ),
        in_specs=[pl.BlockSpec(memory_space=pltpu.SMEM), vmem] + [vmem] * len(seen),
        out_specs=(vmem, vmem),
        scratch_shapes=[
            pltpu.VMEM((count, half, 2 * width), jnp.float32),
            pltpu.VMEM((others if last else 1, 8, 128), jnp.float32),
            pltpu.VMEM((width, early_lanes), jnp.float32),
            pltpu.VMEM((half, 2 * width), jnp.float32),
            pltpu.VMEM((half, 2 * width), jnp.float32),
            pltpu.VMEM((half, share - early_lanes), jnp.float32),
            pltpu.SemaphoreType.DMA((max(count - 1, 1),)),
            pltpu.SemaphoreType.DMA((max(count - 1, 1),)),
            pltpu.SemaphoreType.DMA((max(others - 1, 1),)),
            pltpu.SemaphoreType.DMA((max(others - 1, 1),)),
            pltpu.SemaphoreType.DMA((2 + CHUNKS,)),
            pltpu.SemaphoreType.DMA((2 + CHUNKS,)),
        ],
        compiler_params=pltpu.CompilerParams(
            collective_id=step * (others - 1) + distance - 1, has_side_effects=True),
        name=f"step{step}_by{distance}",
    )(plan, current, *seen)


def place_kernel(plan_ref, current_ref, stat_ref, out_ref, ratio_ref, sems):
    width = current_ref.shape[0]
    half = width // 2
    steps = ratio_ref.shape[0]
    leaving = jnp.where(plan_ref[steps - 1, 1] != 1, 1, 0)
    copies = []
    for index, slot in enumerate((1 - leaving, leaving)):
        copy = pltpu.make_async_copy(
            current_ref.at[pl.ds(index * half, half)],
            out_ref.at[pl.ds(pl.multiple_of(slot * half, half), half)], sems.at[index])
        copy.start()
        copies.append(copy)
    lane = lax.broadcasted_iota(jnp.int32, stat_ref.shape, 1)
    line = lax.broadcasted_iota(jnp.int32, stat_ref.shape, 0)
    values = stat_ref[...]
    for index in range(steps):
        ratio_ref[index] = jnp.sum(jnp.where((lane == index) & (line == 0), values, 0.0))
    for copy in copies:
        copy.wait()


def shift_kernel(plan_ref, *shift_refs):
    for step, shift_ref in enumerate(shift_refs):
        shift_ref[0] = jnp.maximum(plan_ref[step, 0] >> 1, plan_ref[step, 1] >> 1) - 1


def shift_call(plan):
    smem = pl.BlockSpec(memory_space=pltpu.SMEM)
    steps = plan.shape[0]
    return pl.pallas_call(
        shift_kernel,
        out_shape=tuple(jax.ShapeDtypeStruct((1,), jnp.int32) for _ in range(steps)),
        in_specs=[smem],
        out_specs=(smem,) * steps,
        name="shift",
    )(plan)


def local(columns, plan):
    steps = plan.shape[0]
    count = lax.axis_size("blk")
    current = columns
    seen = ()
    shifts = shift_call(plan)
    for step in range(steps):
        branches = [partial(step_call, step=step, last=step == steps - 1, distance=d) for d in range(1, count)]
        current, stat = lax.switch(shifts[step].reshape(()), branches, plan, current, *seen)
        seen = (stat,)
    vmem = pl.BlockSpec(memory_space=pltpu.VMEM)
    return pl.pallas_call(
        place_kernel,
        out_shape=(
            jax.ShapeDtypeStruct(columns.shape, jnp.float32),
            jax.ShapeDtypeStruct((steps,), jnp.float32),
        ),
        in_specs=[pl.BlockSpec(memory_space=pltpu.SMEM), vmem, vmem],
        out_specs=(pl.BlockSpec(memory_space=pl.ANY), pl.BlockSpec(memory_space=pltpu.SMEM)),
        scratch_shapes=[pltpu.SemaphoreType.DMA((2,))],
        name="place",
    )(plan, current, stat)


def solution(mesh):
    return jax.shard_map(
        local,
        mesh=mesh,
        in_specs=(P("blk", "rows"), P()),
        out_specs=(P("blk", "rows"), P()),
        check_vma=False,
    )
```

profile of v0, /device:TPU:0, one launch (start us, length us, event | category | flops | bytes accessed | tf_op | source)
XLA Modules:
  0.0 90.7 jit_solution(1333338350535852067)
XLA Ops:
  0.6 1.2 %shift.1 = (s32[1]{0:T(128)}, s32[1]{0:T(128)}, s32[1]{0:T(128)}) custom-call(s32[3,16]{1,0:T(4,128)} %plan_ref.3), custom_call_target="tpu_custom_call" | custom-call | tf_op jit(solution)/shard_map/shift/pallas_call | solution.py:270
  3.2 0.0 copy-start
  3.9 0.0 copy-done
  3.9 25.0 %conditional.3 = ((f32[64,4096]{1,0:T(8,128)S(1)}, f32[8,128]{1,0:T(8,128)S(1)})) conditional(s32[]{:T(128)} %bitcast.2, (s32[3,16]{1,0:T(4,128)S(1)}, f32[64,4096]{1,0:T(8,128)}) %tuple.115, (s32[3,16]{1,0:T(4,128)S(1)}, f32[64,4096]{1,0:T(8,128)}) %tuple.116, (s32[3,16]{1,0:T(4,128)S(1)}, ...), branch_computations={%region_0.0_spmd, %region_1.0_spmd, %region_2.0_spmd, %region_3.0_... | conditional | bytes 8 | solution.py:287
  3.9 25.0 %step0_by6.1 = (f32[64,4096]{1,0:T(8,128)S(1)}, f32[8,128]{1,0:T(8,128)S(1)}) custom-call(s32[3,16]{1,0:T(4,128)S(1)} %get-tuple-element.122.plan_ref, f32[64,4096]{1,0:T(8,128)} %get-tuple-element.123.current_ref), custom_call_target="tpu_custom_call" | custom-call | tf_op jit(solution)/shard_map/cond/branch_5_fun/step0_by6/pallas_call | solution.py:213
  28.9 34.7 %conditional.4 = ((f32[64,4096]{1,0:T(8,128)S(1)}, f32[8,128]{1,0:T(8,128)S(1)})) conditional(s32[]{:T(128)} %bitcast.1, (s32[3,16]{1,0:T(4,128)S(1)}, f32[64,4096]{1,0:T(8,128)S(1)}, f32[8,128]{1,0:T(8,128)S(1)}) %tuple.122, (s32[3,16]{1,0:T(4,128)S(1)}, f32[64,4096]{1,0:T(8,128)S(1)}, ...), branch_computations={%region_7.0_spmd, %region_8.0_spmd, %region_9.0_spmd, %region_10.0... | conditional | bytes 8 | solution.py:287
  29.2 34.4 %step1_by4.1 = (f32[64,4096]{1,0:T(8,128)S(1)}, f32[8,128]{1,0:T(8,128)S(1)}) custom-call(s32[3,16]{1,0:T(4,128)S(1)} %get-tuple-element.135.plan_ref, f32[64,4096]{1,0:T(8,128)S(1)} %get-tuple-element.136.current_ref, f32[8,128]{1,0:T(8,128)S(1)} %get-tuple-element.137.refs_0_), custom_call_target="tpu_custom_call" | custom-call | tf_op jit(solution)/shard_map/cond/branch_3_fun/step1_by4/pallas_call | solution.py:213
  63.6 24.8 %conditional.5 = ((f32[64,4096]{1,0:T(8,128)S(1)}, f32[8,128]{1,0:T(8,128)S(1)})) conditional(s32[]{:T(128)} %bitcast, (s32[3,16]{1,0:T(4,128)S(1)}, f32[64,4096]{1,0:T(8,128)S(1)}, f32[8,128]{1,0:T(8,128)S(1)}) %tuple.129, (s32[3,16]{1,0:T(4,128)S(1)}, f32[64,4096]{1,0:T(8,128)S(1)}, ...), branch_computations={%region_14.0_spmd, %region_15.0_spmd, %region_16.0_spmd, %region_1... | conditional | bytes 8 | solution.py:287
  63.7 24.4 %step2_by2.1 = (f32[64,4096]{1,0:T(8,128)S(1)}, f32[8,128]{1,0:T(8,128)S(1)}) custom-call(s32[3,16]{1,0:T(4,128)S(1)} %get-tuple-element.150.plan_ref, f32[64,4096]{1,0:T(8,128)S(1)} %get-tuple-element.151.current_ref, f32[8,128]{1,0:T(8,128)S(1)} %get-tuple-element.152.refs_0_), custom_call_target="tpu_custom_call" | custom-call | tf_op jit(solution)/shard_map/cond/branch_1_fun/step2_by2/pallas_call | solution.py:213
  88.4 2.1 %place.1 = (f32[64,4096]{1,0:T(8,128)}, f32[3]{0:T(128)}) custom-call(s32[3,16]{1,0:T(4,128)S(1)} %copy-done, f32[64,4096]{1,0:T(8,128)S(1)} %get-tuple-element.186.current_ref, f32[8,128]{1,0:T(8,128)S(1)} %get-tuple-element.187.stat_ref), custom_call_target="tpu_custom_call" | custom-call | tf_op jit(solution)/shard_map/place/pallas_call | solution.py:290
Async XLA Ops:
  3.2 0.7 copy-start
where the time goes:
time: 91.2 us; the launch traced here: 90.7 us
  Pallas kernels  87.1 us (96%)
  between operations  2.92 us (3%)
    pallas_call x3, Pallas kernels, step_call(): pl.pallas_call(partial(step_kernel, step, last, distance), out_shape=(jax...  83.8 us
    pallas_call x1, Pallas kernels, local(): pl.pallas_call(place_kernel, out_shape=(jax.ShapeDtypeStruct(columns.shap...  2.07 us

commit v1 on v0

v1 whole, which is shorter than its diff:
```python
from functools import partial

import jax
import jax.numpy as jnp
from jax import lax
from jax.experimental import pallas as pl
from jax.experimental.pallas import tpu as pltpu
from jax.sharding import PartitionSpec as P

EIG_ITERS = 3
NS_ITERS = 8
UNROLLED = 8
MESH = pl.DeviceIdType.MESH
(EXCHANGE, EXCHANGE_LATE, TURN0, DIAG0, PARTS, CROSS, LEAD1, DIAG1, STAY1, TURN2, STATS,
 SPREAD, SPREAD_MORE, MIRROR, MIRROR_MORE, NEAR, NEAR_MORE, FAR) = range(18)
BLK_PHASES = 18
ROW_SUMS = 3
ROW_PHASES = 4


def split(value):
    high = value.astype(jnp.bfloat16)
    low = (value - high.astype(jnp.float32)).astype(jnp.bfloat16)
    return high, low


def left_of(value):
    high = value.astype(jnp.bfloat16).astype(jnp.float32)
    low = value - high
    lane = lax.broadcasted_iota(jnp.int32, value.shape, 1)
    mixed = jnp.where(lane < value.shape[1] // 2, high, low).astype(jnp.bfloat16)
    return jnp.concatenate([mixed, mixed], axis=1)


def right_of(value):
    high, low = split(value)
    return jnp.concatenate([high, high, low, low], axis=0)


def turned_right_of(value):
    high, low = split(value)
    both = jnp.concatenate([high, low], axis=1)
    return jnp.concatenate([both, both], axis=0)


def dot(left, right):
    return jnp.dot(left, right, preferred_element_type=jnp.float32)


def dot_turned(left, right):
    return lax.dot_general(left, right, (((1,), (1,)), ((), ())), preferred_element_type=jnp.float32)


def cross_gram(first, second):
    width = first.shape[0]
    left = jnp.concatenate(split(first), axis=0)
    right = left if second is first else jnp.concatenate(split(second), axis=0)
    products = dot_turned(left, right)
    folded = products + pltpu.roll(products, width, 1)
    return folded[:width] + folded[width:]


def lane_of(value):
    return lax.broadcasted_iota(jnp.int32, value.shape, 1)


def pack(value):
    half = value.shape[0] // 2
    top = value[:half]
    return jnp.where(lane_of(top) < value.shape[1] // 2, top, value[half:])


def unpack(packed):
    width = packed.shape[1] // 2
    turned = pltpu.roll(packed, width, 1)
    first = lane_of(packed) < width
    return jnp.where(first, packed, turned), jnp.where(first, turned, packed)


def block_cross(first, second):
    half = first.shape[0]
    high, low = split(second)
    right = jnp.concatenate([high, low, high, low], axis=0)
    products = dot_turned(jnp.concatenate(split(first), axis=0), right)
    folded = products + pltpu.roll(products, half, 1)
    return folded[:half] + folded[half:]


def pack_block(value):
    half, across = value.shape
    groups = across // half
    rows = half // groups
    packed = value[:rows]
    for index in range(1, groups):
        packed = jnp.where(lane_of(packed) < index * half, packed, value[index * rows:(index + 1) * rows])
    return packed


def unpack_block(packed, half):
    groups = packed.shape[1] // half
    lane = lane_of(packed)
    rows = []
    for index in range(groups):
        value = jnp.where((lane >= index * half) & (lane < (index + 1) * half), packed, 0.0)
        reach = half
        while reach < packed.shape[1]:
            value = value + pltpu.roll(value, reach, 1)
            reach *= 2
        rows.append(value)
    return jnp.concatenate(rows, axis=0)


def flip_block(value):
    half, across = value.shape
    return jnp.concatenate([value] * (across // half), axis=0).T[:half]


def orthonormal(z, zt):
    y = z / jnp.sqrt(jnp.sum(z * z, axis=0, keepdims=True))
    t = zt / jnp.sqrt(0.5 * jnp.sum(zt * zt, axis=1, keepdims=True))
    inner = dot(left_of(t), right_of(y))
    bound = jnp.max(jnp.sum(jnp.abs(inner), axis=0, keepdims=True), axis=1, keepdims=True)
    root = jnp.sqrt(bound)
    y = y / root
    t = t / root

    def finish(y, t, inner):
        y_next = 1.5 * y - 0.5 * dot(left_of(y), right_of(inner))
        t_next = 1.5 * t - 0.5 * dot(left_of(inner), right_of(t))
        return y_next, t_next

    def turn(_, carry):
        y, t = carry
        return finish(y, t, dot(left_of(t), right_of(y)))

    return lax.fori_loop(1, NS_ITERS, turn, finish(y, t, inner / bound))


def pair_rotation(gram):
    q, t = orthonormal(gram, gram)
    gram_left, gram_right = left_of(gram), right_of(gram)

    def again(_, carry):
        q, t = carry
        return orthonormal(dot(gram_left, right_of(q)), dot(left_of(t), gram_right))

    return lax.fori_loop(1, EIG_ITERS, again, (q, t))[1]


def each(count, body):
    if count <= UNROLLED:
        for index in range(count):
            body(index)
    else:
        def loop(index, carry):
            body(index)
            return carry
        lax.fori_loop(0, count, loop, 0)


def totals(gram, seen, step):
    width = gram.shape[0]
    row = lax.broadcasted_iota(jnp.int32, gram.shape, 0)
    column = lane_of(gram)
    square = gram * gram
    diag_part = jnp.where(row == column, square, 0.0)
    off_part = jnp.where((row == column) | (column >= width), 0.0, square)
    off_total = jnp.sum(jnp.sum(off_part, axis=0, keepdims=True), axis=1, keepdims=True)
    diag_total = jnp.sum(jnp.sum(diag_part, axis=0, keepdims=True), axis=1, keepdims=True)
    line = lax.broadcasted_iota(jnp.int32, seen.shape, 0)
    fresh = jnp.where(line == 0, off_total, diag_total)
    return jnp.where((lane_of(seen) == step) & (line < 2), fresh, seen)


def doubled(lanes):
    return lanes // 2 // 256 * 256


def kernel(plan_hbm, columns_ref, out_ref, stat_ref,
           plan_ref, columns, raw, turned, paired, ready, extra_raw, extra, extra_paired, own_turn, quarters, leads, stays, last_turns,
           parts, part_in, part_sums, diags, more_diags, crosses, cross_in, sums, stats,
           plan_sem, fetch_sem, blk_send, blk_recv, row_send, row_recv):
    width, share = columns.shape
    half = width // 2
    count = lax.axis_size("rows")
    others = lax.axis_size("blk")
    me = lax.axis_index("rows")
    mine = lax.axis_index("blk")
    lanes = share // others
    early = lanes // 2 // 128 * 128
    quarter = quarters.shape[2]
    shared = doubled(lanes)
    kept = lanes - shared
    group = others // 2
    base = mine // group * group
    mirror_base = group - base
    place = mine - base
    far_first = sorted(range(1, others), key=lambda offset: (abs(2 * offset - others), offset))

    fetch = pltpu.make_async_copy(columns_ref, columns, fetch_sem)
    fetch.start()
    plan_fetch = pltpu.make_async_copy(plan_hbm, plan_ref, plan_sem)
    plan_fetch.start()
    barrier = pltpu.get_barrier_semaphore()
    for offset in range(1, count):
        pl.semaphore_signal(barrier, inc=1, device_id={"rows": lax.rem(me + offset, count)}, device_id_type=MESH)
    for offset in range(1, others):
        pl.semaphore_signal(barrier, inc=1, device_id={"blk": lax.rem(mine + offset, others)}, device_id_type=MESH)

    def peer_of(offset):
        return lax.rem(mine + offset, others)

    def send(phase, slot, peer, src, dst):
        copy = pltpu.make_async_remote_copy(
            src_ref=src, dst_ref=dst,
            send_sem=blk_send.at[phase, slot], recv_sem=blk_recv.at[phase, slot],
            device_id={"blk": peer}, device_id_type=MESH)
        copy.start()
        return copy

    def blk_copy(phase, offset, src, dst):
        return send(phase, offset - 1, peer_of(offset), src, dst)

    def near_peer(offset):
        return base + lax.rem(place + offset, group)

    def far_peer(offset):
        return mirror_base + lax.rem(place + offset, group)

    def gather(phase, ref):
        return [blk_copy(phase, offset, ref.at[mine], ref.at[mine]) for offset in far_first]

    def scatter(phase, src_ref, dst_ref):
        return [blk_copy(phase, offset, src_ref.at[peer_of(offset)], dst_ref.at[mine]) for offset in far_first]

    def exchange(phase, src_ref, start, size):
        copies = []
        for offset in far_first:
            lane_start = pl.multiple_of(peer_of(offset) * lanes + start, 128)
            copies.append(blk_copy(phase, offset, src_ref.at[:, pl.ds(lane_start, size)],
                                   raw.at[mine, :, pl.ds(start, size)]))
        return copies

    def finish(copies):
        for copy in copies:
            copy.wait()

    def total_of(ref):
        total = ref[0]
        for index in range(1, ref.shape[0]):
            total = total + ref[index]
        return total

    def share_rows(phase, ref):
        copies = []
        for offset in range(1, count):
            copy = pltpu.make_async_remote_copy(
                src_ref=ref.at[me], dst_ref=ref.at[me],
                send_sem=row_send.at[phase, offset - 1], recv_sem=row_recv.at[phase, offset - 1],
                device_id={"rows": lax.rem(me + offset, count)}, device_id_type=MESH)
            copy.start()
            copies.append(copy)
        return copies

    def start_rows(phase, packed):
        sums[phase, me] = packed
        return share_rows(phase, sums.at[phase])

    def end_rows(phase, copies):
        finish(copies)
        return total_of(sums.at[phase])

    def source(step, slot, pair):
        return lax.rem(pair + others - (plan_ref[step, slot] >> 1), others)

    def partner(step):
        return lax.rem(mine + others - (plan_ref[step, 0] >> 1) - (plan_ref[step, 1] >> 1), others)

    def placed(ref, step, pair, where=slice(None)):
        return jnp.concatenate([ref[source(step, 0, pair), pl.ds(0, half), where],
                                ref[source(step, 1, pair), pl.ds(half, half), where]], axis=0)

    def whole(packed):
        return jnp.concatenate(unpack(packed), axis=0)

    low_lane = (lax.broadcasted_iota(jnp.int32, (half, 2 * width), 1) & (width - 1)) < half
    def rotated_diag(turn, gram, first_leaves):
        rotated = dot_turned(left_of(dot(left_of(turn), right_of(gram))), turned_right_of(turn))
        first, second = rotated[:half], rotated[half:]
        leaving = jnp.where(first_leaves,
                            jnp.where(low_lane, first, pltpu.roll(first, half, 1)),
                            jnp.where(low_lane, pltpu.roll(second, half, 1), second))
        return first, second, pack_block(leaving)

    def spread(more):
        size = shared // 2
        start = kept + more * size
        into = pl.ds(more * size, size)
        copies = []
        for offset in range(1, group):
            peer = near_peer(offset)
            mirrored = mirror_base + peer - base
            lane_start = pl.multiple_of(mirrored * lanes + start, 128)
            copies.append(send(SPREAD + more, offset - 1, peer, columns.at[:, pl.ds(lane_start, size)],
                               extra_raw.at[mine, :, into]))
        copies.append(send(MIRROR + more, 0, mirror_base + place, raw.at[pl.ds(base, group), :, pl.ds(start, size)],
                           extra_raw.at[pl.ds(base, group), :, into]))
        lane_start = pl.multiple_of((mirror_base + place) * lanes + start, 128)
        extra_raw[mine, :, into] = columns[:, pl.ds(lane_start, size)]
        return copies

    pl.semaphore_wait(barrier, count - 1 + others - 1)
    early_copies = exchange(EXCHANGE, columns_ref, 0, early) if early else []
    fetch.wait()
    value = columns[...]
    gram = cross_gram(value, value)
    row_copies = start_rows(0, pack(gram))
    raw[mine] = columns[:, pl.ds(pl.multiple_of(mine * lanes, 128), lanes)]
    plan_fetch.wait()

    gram = whole(end_rows(0, row_copies))
    seen = totals(gram, jnp.zeros(stats.shape[1:], jnp.float32), 0)
    turn = pair_rotation(gram)
    own_turn[...] = pack(turn)
    my_quarter = pl.ds(pl.multiple_of(me * quarter, quarter), quarter)
    turn_copies = [blk_copy(TURN0, offset, own_turn.at[my_quarter], quarters.at[me, mine]) for offset in far_first]
    late_copies = exchange(EXCHANGE_LATE, columns, early, lanes - early)
    first_leaves = (plan_ref[0, 0] >> 1) > 0
    first_diag, second_diag, diags[mine] = rotated_diag(turn, gram, first_leaves)
    diag_copies = gather(DIAG0, diags)
    quarters[me, mine] = own_turn[my_quarter]
    finish(turn_copies)
    turn_rows = share_rows(ROW_SUMS, quarters)
    finish(turn_rows)

    def first_turn_of(pair):
        return whole(jnp.concatenate([quarters[index, pair] for index in range(count)], axis=0))

    def first_turn(start, size):
        def body(pair):
            where = pl.ds(start, size)
            turned[pair, :, where] = dot(left_of(first_turn_of(pair)), right_of(raw[pair, :, where]))
        each(others, body)

    finish(early_copies)
    if early:
        first_turn(0, early)
    finish(late_copies)
    first_turn(early, lanes - early)

    def pair_gram(pair):
        value = placed(turned, 0, pair)
        paired[pair] = value
        parts[pair] = pack_block(block_cross(value[:half], value[half:]))

    each(others, pair_gram)
    part_copies = scatter(PARTS, parts, part_in)
    part_in[mine] = parts[mine]

    def pair_cross(pair):
        crosses[pair] = pack(cross_gram(paired[source(1, 0, pair)], paired[source(1, 1, pair)]))

    each(others, pair_cross)
    cross_in[mine] = crosses[mine]

    finish(part_copies)
    part_sums[me] = total_of(part_in)
    row_copies = share_rows(1, part_sums)
    cross_copies = scatter(CROSS, crosses, cross_in)
    finish(diag_copies)
    from_other = unpack_block(diags[partner(0)], half)
    finish(row_copies)
    block = unpack_block(total_of(part_sums), half)
    gram = jnp.concatenate([
        jnp.where(low_lane, jnp.where(first_leaves, from_other, first_diag), block),
        jnp.where(low_lane, flip_block(block), jnp.where(first_leaves, second_diag, from_other))], axis=0)
    spread_copies = spread(0) if shared else []
    seen = totals(gram, seen, 1)
    turn = pair_rotation(gram)
    first_leaves = (plan_ref[1, 0] >> 1) > 0
    lead = jnp.where(first_leaves, turn[:half], turn[half:])
    stay = jnp.where(first_leaves, turn[half:], turn[:half])
    leads[mine] = pack(lead)
    lead_copies = gather(LEAD1, leads)
    stays[mine] = pack(stay)
    first_diag, second_diag, more_diags[mine] = rotated_diag(turn, gram, first_leaves)
    diag_copies = gather(DIAG1, more_diags)
    finish(cross_copies)
    cross_rows = start_rows(2, total_of(cross_in))
    cross = whole(end_rows(2, cross_rows))
    cross_right, cross_turned = right_of(cross), turned_right_of(cross)
    finish(lead_copies)
    from_other = whole(leads[partner(1)])
    first_turns = jnp.where(first_leaves, from_other, stay)
    second_turns = jnp.where(first_leaves, stay, from_other)
    inner = jnp.concatenate([dot(left_of(first_turns), cross_right),
                             dot_turned(left_of(second_turns), cross_turned)], axis=0)
    outer = dot_turned(left_of(inner), turned_right_of(jnp.concatenate([first_turns, second_turns], axis=0)))
    finish(diag_copies)
    stay_copies = gather(STAY1, stays)
    finish(spread_copies)
    spread_copies = spread(1) if shared else []
    from_other = unpack_block(more_diags[partner(1)], half)
    gram = jnp.concatenate([
        jnp.where(low_lane, jnp.where(first_leaves, from_other, first_diag), outer[:half]),
        jnp.where(low_lane, outer[half:], jnp.where(first_leaves, second_diag, from_other))], axis=0)
    stats[mine] = totals(gram, seen, 2)
    stat_copies = gather(STATS, stats)
    last_turns[mine] = pack(pair_rotation(gram))
    turn_copies = gather(TURN2, last_turns)

    finish(stay_copies)

    def second_turn_of(pair):
        lead, stay = whole(leads[pair]), whole(stays[pair])
        return left_of(jnp.concatenate([jnp.where(first_leaves, lead, stay),
                                        jnp.where(first_leaves, stay, lead)], axis=0))

    def second_turn(pair):
        ready[pair] = dot(second_turn_of(pair), right_of(paired[pair]))

    each(others, second_turn)

    def pair_again(pair):
        paired[pair] = placed(ready, 1, pair)

    each(others, pair_again)
    finish(spread_copies)
    if shared:
        def extra_first(pair):
            extra[pair] = dot(left_of(first_turn_of(pair)), right_of(extra_raw[pair]))

        def extra_pair(pair):
            extra_paired[pair] = placed(extra, 0, pair)

        def extra_second(pair):
            extra_raw[pair] = dot(second_turn_of(pair), right_of(extra_paired[pair]))

        def extra_again(pair):
            extra_paired[pair] = placed(extra_raw, 1, pair)

        each(others, extra_first)
        each(others, extra_pair)
        each(others, extra_second)
        each(others, extra_again)
    finish(stat_copies)
    total = total_of(stats)
    stat_ref[...] = jnp.broadcast_to(jnp.sqrt(total[0:1]) / jnp.sqrt(total[1:2]), stat_ref.shape)
    finish(turn_copies)

    def last_turn(pair, ref, size):
        first, second = source(2, 0, pair), source(2, 1, pair)
        where = pl.ds(0, size)
        upper = dot(left_of(unpack(last_turns[first])[0]), right_of(ref[first, :, where]))
        lower = dot(left_of(unpack(last_turns[second])[1]), right_of(ref[second, :, where]))
        return jnp.concatenate([upper, lower], axis=0)

    def lanes_at(chunk, start, size):
        return pl.ds(pl.multiple_of(chunk * lanes + start, 128), size)

    back = []
    for offset in range(group):
        peer = far_peer(offset)
        turned[peer, :, pl.ds(0, kept)] = last_turn(peer, paired, kept)
        back.append(send(FAR, offset, peer, turned.at[peer, :, pl.ds(0, kept)], out_ref.at[:, lanes_at(mine, 0, kept)]))
    mirror = mirror_base + place
    for offset in list(range(1, group)) + [0]:
        peer = near_peer(offset)
        result = last_turn(peer, paired, lanes)
        if offset:
            turned[peer] = result
            back.append(send(NEAR, offset - 1, peer, turned.at[peer], out_ref.at[:, lanes_at(mine, 0, lanes)]))
        else:
            out_ref[:, lanes_at(mine, 0, lanes)] = result
        if shared:
            result = last_turn(peer, extra_paired, shared)
            if offset:
                extra[peer] = result
                back.append(send(NEAR_MORE, offset - 1, peer, extra.at[peer],
                                 out_ref.at[:, lanes_at(mirror, kept, shared)]))
            else:
                out_ref[:, lanes_at(mirror, kept, shared)] = result
    finish(back)


def place_kernel(current_ref, stat_ref, out_ref, ratio_ref, sems):
    width = current_ref.shape[0]
    pieces = sems.shape[0]
    size = width // pieces
    copies = []
    for index in range(pieces):
        where = pl.ds(index * size, size)
        copy = pltpu.make_async_copy(current_ref.at[where], out_ref.at[where], sems.at[index])
        copy.start()
        copies.append(copy)
    line = lax.broadcasted_iota(jnp.int32, stat_ref.shape, 0)
    values = stat_ref[...]
    for index in range(ratio_ref.shape[0]):
        ratio_ref[index] = jnp.sum(jnp.where((lane_of(values) == index) & (line == 0), values, 0.0))
    for copy in copies:
        copy.wait()


def local(columns, plan):
    width, share = columns.shape
    half = width // 2
    steps = plan.shape[0]
    count = lax.axis_size("rows")
    others = lax.axis_size("blk")
    lanes = share // others
    smem = pl.BlockSpec(memory_space=pltpu.SMEM)
    vmem = pl.BlockSpec(memory_space=pltpu.VMEM)
    hbm = pl.BlockSpec(memory_space=pl.ANY)
    stored = pl.BlockSpec(memory_space=pltpu.HBM)
    wide = pltpu.VMEM((others, width, lanes), jnp.float32)
    more = pltpu.VMEM((others, width, max(doubled(lanes), 128)), jnp.float32)
    small = pltpu.VMEM((others, half, 2 * width), jnp.float32)
    smaller = pltpu.VMEM((others, half // 2, 2 * width), jnp.float32)
    block = pltpu.VMEM((others, half * half // (2 * width), 2 * width), jnp.float32)
    current, stat = pl.pallas_call(
        kernel,
        out_shape=(
            jax.ShapeDtypeStruct(columns.shape, jnp.float32),
            jax.ShapeDtypeStruct((8, 128), jnp.float32),
        ),
        in_specs=[stored, stored],
        out_specs=(vmem, vmem),
        scratch_shapes=[
            pltpu.SMEM(plan.shape, jnp.int32),
            pltpu.VMEM((width, share), jnp.float32),
            wide, wide, wide, wide,
            more, more, more,
            pltpu.VMEM((half, 2 * width), jnp.float32),
            pltpu.VMEM((count, others, half // count, 2 * width), jnp.float32),
            smaller, smaller, small,
            block, block, pltpu.VMEM((count,) + block.shape[1:], jnp.float32), block, block,
            small, small,
            pltpu.VMEM((ROW_SUMS, count, half, 2 * width), jnp.float32),
            pltpu.VMEM((others, 8, 128), jnp.float32),
            pltpu.SemaphoreType.DMA,
            pltpu.SemaphoreType.DMA,
            pltpu.SemaphoreType.DMA((BLK_PHASES, max(others - 1, 1))),
            pltpu.SemaphoreType.DMA((BLK_PHASES, max(others - 1, 1))),
            pltpu.SemaphoreType.DMA((ROW_PHASES, max(count - 1, 1))),
            pltpu.SemaphoreType.DMA((ROW_PHASES, max(count - 1, 1))),
        ],
        compiler_params=pltpu.CompilerParams(collective_id=0, has_side_effects=True, vmem_limit_bytes=24 << 20),
        name="steps",
    )(plan, columns)
    return pl.pallas_call(
        place_kernel,
        out_shape=(
            jax.ShapeDtypeStruct(columns.shape, jnp.float32),
            jax.ShapeDtypeStruct((steps,), jnp.float32),
        ),
        in_specs=[vmem, vmem],
        out_specs=(hbm, smem),
        scratch_shapes=[pltpu.SemaphoreType.DMA((8,))],
        compiler_params=pltpu.CompilerParams(vmem_limit_bytes=8 << 20),
        name="place",
    )(current, stat)


def solution(mesh):
    return jax.shard_map(
        local,
        mesh=mesh,
        in_specs=(P("blk", "rows"), P()),
        out_specs=(P("blk", "rows"), P()),
        check_vma=False,
    )
```

time: 91.2 us -> 85.7 us (0.940)
  Pallas kernels: 87.1 us -> 83 us
  between operations: 2.92 us -> 0.65 us
  local copies, waits for them, and re-layouts: 0.01 us -> 1.9 us
    pallas_call x4 -> x1, Pallas kernels: 85 us -> 81.5 us  [local(): pl.pallas_call(kernel, out_shape=(jax.ShapeDtypeStruct(columns.shape, jnp...]
    unnamed x2 -> x4, local copies, waits for them, and re-layouts: 0.01 us -> 1.9 us
where the time goes in v1:
time: 85.7 us; the launch traced here: 85.5 us
  Pallas kernels  83 us (97%)
  local copies, waits for them, and re-layouts  1.9 us (2%)
    pallas_call x1, Pallas kernels, local(): pl.pallas_call(kernel, out_shape=(jax.ShapeDtypeStruct(columns.shape, jnp...  81.5 us
    unnamed x4, local copies, waits for them, and re-layouts  1.9 us

profile of v1, /device:TPU:0, one launch (start us, length us, event | category | flops | bytes accessed | tf_op | source)
XLA Modules:
  0.0 85.5 jit_solution(46817016165746090)
XLA Ops:
  0.6 0.0 copy-start
  0.6 1.2 %copy-done = f32[64,4096]{1,0:T(8,128)S(1)} copy-done((f32[64,4096]{1,0:T(8,128)S(1)}, f32[64,4096]{1,0:T(8,128)}, u32[]{:S(2)}) %copy-start) | copy-done | bytes 1048600
  1.9 0.0 copy-start.1
  1.9 0.7 copy-done.1
  2.5 81.5 %steps.1 = (f32[64,4096]{1,0:T(8,128)S(1)}, f32[8,128]{1,0:T(8,128)S(1)}) custom-call(s32[3,16]{1,0:T(4,128)S(1)} %copy-done.1, f32[64,4096]{1,0:T(8,128)S(1)} %copy-done), custom_call_target="tpu_custom_call" | custom-call | tf_op jit(solution)/shard_map/steps/pallas_call | solution.py:520
  84.0 1.5 %place.1 = (f32[64,4096]{1,0:T(8,128)}, f32[3]{0:T(128)}) custom-call(f32[64,4096]{1,0:T(8,128)S(1)} %get-tuple-element.4.current_ref, f32[8,128]{1,0:T(8,128)S(1)} %get-tuple-element.5.stat_ref), custom_call_target="tpu_custom_call" | custom-call | tf_op jit(solution)/shard_map/place/pallas_call | solution.py:550
Async XLA Ops:
  0.6 1.2 %copy-start = (f32[64,4096]{1,0:T(8,128)S(1)}, f32[64,4096]{1,0:T(8,128)}, u32[]{:S(2)}) copy-start(f32[64,4096]{1,0:T(8,128)} %columns_ref.1) | copy-start | bytes 3145732
  1.9 0.7 copy-start.1

commit v2 on v1

--- a/solution.py
+++ b/solution.py
@@ -10,6 +10,7 @@
 EIG_ITERS = 3
 NS_ITERS = 8
 UNROLLED = 8
+AHEAD = 1
 MESH = pl.DeviceIdType.MESH
 (EXCHANGE, EXCHANGE_LATE, TURN0, DIAG0, PARTS, CROSS, LEAD1, DIAG1, STAY1, TURN2, STATS,
  SPREAD, SPREAD_MORE, MIRROR, MIRROR_MORE, NEAR, NEAR_MORE, FAR) = range(18)
@@ -115,7 +116,7 @@
     return jnp.concatenate([value] * (across // half), axis=0).T[:half]
 
 
-def orthonormal(z, zt):
+def orthonormal(z, zt, gram_left, gram_right):
     y = z / jnp.sqrt(jnp.sum(z * z, axis=0, keepdims=True))
     t = zt / jnp.sqrt(0.5 * jnp.sum(zt * zt, axis=1, keepdims=True))
     inner = dot(left_of(t), right_of(y))
@@ -129,22 +130,22 @@
         t_next = 1.5 * t - 0.5 * dot(left_of(inner), right_of(t))
         return y_next, t_next
 
-    def turn(_, carry):
-        y, t = carry
-        return finish(y, t, dot(left_of(t), right_of(y)))
-
-    return lax.fori_loop(1, NS_ITERS, turn, finish(y, t, inner / bound))
+    y, t = finish(y, t, inner / bound)
+    for _ in range(2, NS_ITERS):
+        y, t = finish(y, t, dot(left_of(t), right_of(y)))
+    inner = dot(left_of(t), right_of(y))
+    return y, t, inner, finish(dot(gram_left, right_of(y)), dot(left_of(t), gram_right), inner)
 
 
 def pair_rotation(gram):
-    q, t = orthonormal(gram, gram)
     gram_left, gram_right = left_of(gram), right_of(gram)
 
     def again(_, carry):
-        q, t = carry
-        return orthonormal(dot(gram_left, right_of(q)), dot(left_of(t), gram_right))
-
-    return lax.fori_loop(1, EIG_ITERS, again, (q, t))[1]
+        return orthonormal(*carry, gram_left, gram_right)[3]
+
+    z, zt = lax.fori_loop(1, EIG_ITERS, again, (gram, gram))
+    y, t, inner, _ = orthonormal(z, zt, gram_left, gram_right)
+    return 1.5 * t - 0.5 * dot(left_of(inner), right_of(t))
 
 
 def each(count, body):
@@ -227,18 +228,21 @@
     def far_peer(offset):
         return mirror_base + lax.rem(place + offset, group)
 
+    far_peers = [(offset, far_peer(offset)) for offset in range(group)]
+    near_peers = [(group + offset - 1, near_peer(offset)) for offset in range(1, group)]
+
     def gather(phase, ref):
         return [blk_copy(phase, offset, ref.at[mine], ref.at[mine]) for offset in far_first]
 
     def scatter(phase, src_ref, dst_ref):
         return [blk_copy(phase, offset, src_ref.at[peer_of(offset)], dst_ref.at[mine]) for offset in far_first]
 
-    def exchange(phase, src_ref, start, size):
+    def exchange(phase, peers, src_ref, start, size):
         copies = []
-        for offset in far_first:
-            lane_start = pl.multiple_of(peer_of(offset) * lanes + start, 128)
-            copies.append(blk_copy(phase, offset, src_ref.at[:, pl.ds(lane_start, size)],
-                                   raw.at[mine, :, pl.ds(start, size)]))
+        for slot, peer in peers:
+            lane_start = pl.multiple_of(peer * lanes + start, 128)
+            copies.append(send(phase, slot, peer, src_ref.at[:, pl.ds(lane_start, size)],
+                               raw.at[mine, :, pl.ds(start, size)]))
         return copies
 
     def finish(copies):
@@ -310,7 +314,9 @@
         return copies
 
     pl.semaphore_wait(barrier, count - 1 + others - 1)
-    early_copies = exchange(EXCHANGE, columns_ref, 0, early) if early else []
+    early_copies = exchange(EXCHANGE, far_peers, columns_ref, 0, early) if early else []
+    late_copies = exchange(EXCHANGE_LATE, far_peers[:AHEAD], columns_ref, early, lanes - early)
+    early_copies += exchange(EXCHANGE, near_peers, columns_ref, 0, early) if early else []
     fetch.wait()
     value = columns[...]
     gram = cross_gram(value, value)
@@ -324,10 +330,9 @@
     own_turn[...] = pack(turn)
     my_quarter = pl.ds(pl.multiple_of(me * quarter, quarter), quarter)
     turn_copies = [blk_copy(TURN0, offset, own_turn.at[my_quarter], quarters.at[me, mine]) for offset in far_first]
-    late_copies = exchange(EXCHANGE_LATE, columns, early, lanes - early)
+    late_copies += exchange(EXCHANGE_LATE, far_peers[AHEAD:] + near_peers, columns, early, lanes - early)
     first_leaves = (plan_ref[0, 0] >> 1) > 0
     first_diag, second_diag, diags[mine] = rotated_diag(turn, gram, first_leaves)
-    diag_copies = gather(DIAG0, diags)
     quarters[me, mine] = own_turn[my_quarter]
     finish(turn_copies)
     turn_rows = share_rows(ROW_SUMS, quarters)
@@ -355,6 +360,7 @@
 
     each(others, pair_gram)
     part_copies = scatter(PARTS, parts, part_in)
+    diag_copies = gather(DIAG0, diags)
     part_in[mine] = parts[mine]
 
     def pair_cross(pair):
@@ -544,7 +550,7 @@
             pltpu.SemaphoreType.DMA((ROW_PHASES, max(count - 1, 1))),
             pltpu.SemaphoreType.DMA((ROW_PHASES, max(count - 1, 1))),
         ],
-        compiler_params=pltpu.CompilerParams(collective_id=0, has_side_effects=True, vmem_limit_bytes=24 << 20),
+        compiler_params=pltpu.CompilerParams(collective_id=0, has_side_effects=True, vmem_limit_bytes=55_000_000),
         name="steps",
     )(plan, columns)
     return pl.pallas_call(

time: 85.7 us -> 83.2 us (0.971)
  Pallas kernels: 83 us -> 81.7 us
  local copies, waits for them, and re-layouts: 1.9 us -> 0.67 us
    pallas_call x1, Pallas kernels: 81.5 us -> 80.2 us  [local(): pl.pallas_call(kernel, out_shape=(jax.ShapeDtypeStruct(columns.shape, jnp...]
    unnamed x4 -> x2, local copies, waits for them, and re-layouts: 1.9 us -> 0.67 us
where the time goes in v2:
time: 83.2 us; the launch traced here: 83 us
  Pallas kernels  81.7 us (98%)
    pallas_call x1, Pallas kernels, local(): pl.pallas_call(kernel, out_shape=(jax.ShapeDtypeStruct(columns.shape, jnp...  80.2 us

profile of v2, /device:TPU:0, one launch (start us, length us, event | category | flops | bytes accessed | tf_op | source)
XLA Modules:
  0.0 83.0 jit_solution(11076992883230905833)
XLA Ops:
  0.6 0.0 copy-start
  0.6 0.7 copy-done
  1.3 80.2 %steps.1 = (f32[64,4096]{1,0:T(8,128)S(1)}, f32[8,128]{1,0:T(8,128)S(1)}) custom-call(s32[3,16]{1,0:T(4,128)S(1)} %copy-done, f32[64,4096]{1,0:T(8,128)} %columns_ref.1), custom_call_target="tpu_custom_call" | custom-call | tf_op jit(solution)/shard_map/steps/pallas_call | solution.py:526
  81.5 1.5 %place.1 = (f32[64,4096]{1,0:T(8,128)}, f32[3]{0:T(128)}) custom-call(f32[64,4096]{1,0:T(8,128)S(1)} %get-tuple-element.4.current_ref, f32[8,128]{1,0:T(8,128)S(1)} %get-tuple-element.5.stat_ref), custom_call_target="tpu_custom_call" | custom-call | tf_op jit(solution)/shard_map/place/pallas_call | solution.py:556
Async XLA Ops:
  0.6 0.7 copy-start

commit v3 on v2

--- a/solution.py
+++ b/solution.py
@@ -552,7 +552,7 @@
         ],
         compiler_params=pltpu.CompilerParams(collective_id=0, has_side_effects=True, vmem_limit_bytes=55_000_000),
         name="steps",
-    )(plan, columns)
+    )(pltpu.with_memory_space_constraint(plan, pltpu.HBM), columns)
     return pl.pallas_call(
         place_kernel,
         out_shape=(

time: 83.2 us -> 82.6 us (level)
  no operation moved by 1% of the time
where the time goes in v3:
time: 82.6 us; the launch traced here: 82.4 us
  Pallas kernels  81.8 us (99%)
    pallas_call x1, Pallas kernels, local(): pl.pallas_call(kernel, out_shape=(jax.ShapeDtypeStruct(columns.shape, jnp...  80.2 us

profile of v3, /device:TPU:0, one launch (start us, length us, event | category | flops | bytes accessed | tf_op | source)
XLA Modules:
  0.0 82.4 jit_solution(14271927678547743995)
XLA Ops:
  0.6 80.2 %steps.1 = (f32[64,4096]{1,0:T(8,128)S(1)}, f32[8,128]{1,0:T(8,128)S(1)}) custom-call(s32[3,16]{1,0:T(4,128)} %plan_hbm.1, f32[64,4096]{1,0:T(8,128)} %columns_ref.1), custom_call_target="tpu_custom_call" | custom-call | tf_op jit(solution)/shard_map/steps/pallas_call | solution.py:526
  80.9 1.5 %place.1 = (f32[64,4096]{1,0:T(8,128)}, f32[3]{0:T(128)}) custom-call(f32[64,4096]{1,0:T(8,128)S(1)} %get-tuple-element.4.current_ref, f32[8,128]{1,0:T(8,128)S(1)} %get-tuple-element.5.stat_ref), custom_call_target="tpu_custom_call" | custom-call | tf_op jit(solution)/shard_map/place/pallas_call | solution.py:556

commit v4 on v3

--- a/solution.py
+++ b/solution.py
@@ -301,14 +301,14 @@
         start = kept + more * size
         into = pl.ds(more * size, size)
         copies = []
+        copies.append(send(MIRROR + more, 0, mirror_base + place, raw.at[pl.ds(base, group), :, pl.ds(start, size)],
+                           extra_raw.at[pl.ds(base, group), :, into]))
         for offset in range(1, group):
             peer = near_peer(offset)
             mirrored = mirror_base + peer - base
             lane_start = pl.multiple_of(mirrored * lanes + start, 128)
             copies.append(send(SPREAD + more, offset - 1, peer, columns.at[:, pl.ds(lane_start, size)],
                                extra_raw.at[mine, :, into]))
-        copies.append(send(MIRROR + more, 0, mirror_base + place, raw.at[pl.ds(base, group), :, pl.ds(start, size)],
-                           extra_raw.at[pl.ds(base, group), :, into]))
         lane_start = pl.multiple_of((mirror_base + place) * lanes + start, 128)
         extra_raw[mine, :, into] = columns[:, pl.ds(lane_start, size)]
         return copies
@@ -404,8 +404,7 @@
     outer = dot_turned(left_of(inner), turned_right_of(jnp.concatenate([first_turns, second_turns], axis=0)))
     finish(diag_copies)
     stay_copies = gather(STAY1, stays)
-    finish(spread_copies)
-    spread_copies = spread(1) if shared else []
+    spread_copies += spread(1) if shared else []
     from_other = unpack_block(more_diags[partner(1)], half)
     gram = jnp.concatenate([
         jnp.where(low_lane, jnp.where(first_leaves, from_other, first_diag), outer[:half]),

time: 82.6 us -> 82.5 us (level)
  no operation moved by 1% of the time
where the time goes in v4:
time: 82.5 us; the launch traced here: 82.4 us
  Pallas kernels  81.7 us (99%)
    pallas_call x1, Pallas kernels, local(): pl.pallas_call(kernel, out_shape=(jax.ShapeDtypeStruct(columns.shape, jnp...  80.2 us

profile of v4, /device:TPU:0, one launch (start us, length us, event | category | flops | bytes accessed | tf_op | source)
XLA Modules:
  0.0 82.4 jit_solution(17543380881466905119)
XLA Ops:
  0.6 80.2 %steps.1 = (f32[64,4096]{1,0:T(8,128)S(1)}, f32[8,128]{1,0:T(8,128)S(1)}) custom-call(s32[3,16]{1,0:T(4,128)} %plan_hbm.1, f32[64,4096]{1,0:T(8,128)} %columns_ref.1), custom_call_target="tpu_custom_call" | custom-call | tf_op jit(solution)/shard_map/steps/pallas_call | solution.py:525
  80.8 1.5 %place.1 = (f32[64,4096]{1,0:T(8,128)}, f32[3]{0:T(128)}) custom-call(f32[64,4096]{1,0:T(8,128)S(1)} %get-tuple-element.4.current_ref, f32[8,128]{1,0:T(8,128)S(1)} %get-tuple-element.5.stat_ref), custom_call_target="tpu_custom_call" | custom-call | tf_op jit(solution)/shard_map/place/pallas_call | solution.py:555
